TPU v7x, 32 devices: a whole 2x2x4 slice. The times are simulated.
32 devices in a mesh: gx: 4 (over z), gy: 8 (over y, x, core).
Axes of the slice: x: 2, y: 2, z: 4, core: 2. Of those that a mesh axis runs over, the one named last changes fastest.
Arguments:
- tokens: bfloat16 [28672, 4096], P(('gx', 'gy')), may hold values from -6 to 6
- codes: bfloat16 [4096, 512], P(('gx', 'gy')), may hold values from -0.09375 to 0.09375
- scales: float32 [128, 4], P(('gx', 'gy')), may hold values from 0.5 to 2
- gain: float32 [128], replicated, may hold values from 0.1 to 1.9
- cotangent: bfloat16 [28672, 512], P(('gx', 'gy')), may hold values from -96 to 96
Outputs:
- keys: bfloat16 [28672, 512], P(('gx', 'gy'))
- token_grad: bfloat16 [28672, 4096], P(('gx', 'gy'))
- weight_grad: float32 [4096, 512], P(('gx', 'gy'))
All inputs are finite; a program needn't handle non-finite values.
Results may differ from a plain program's by a relative error of at most 0.019.
Values may be sent and summed in bfloat16 or wider, within the bound.
No kernel may reach another device: no remote copies, remote signals or barrier semaphores. Data moves between devices by JAX's collectives and lax.ppermute only.
A program may use at most 128 MiB of HBM per device.

v0:
```python
import math
import jax
import jax.numpy as jnp
from jax import lax
from jax.sharding import PartitionSpec as P

KV_HEADS = 4
HEAD = 128
QBLK = 32
clip_ratio = 2.5


def hadamard(length):
    indices = jnp.arange(length, dtype=jnp.int32)
    common = jnp.bitwise_and(indices[:, None], indices[None, :])
    parity = jnp.zeros((length, length), jnp.int32)
    for position in range(length.bit_length() - 1):
        parity = parity + jnp.bitwise_and(jnp.right_shift(common, position), 1)
    return (1 - 2 * (parity % 2)).astype(jnp.float32) / math.sqrt(length)


def rotate(matrix, rotation):
    shaped = matrix.reshape(matrix.shape[0], KV_HEADS, HEAD)
    rotated = jnp.einsum("rhc,cd->rhd", shaped, rotation, precision=lax.Precision.HIGHEST)
    return rotated.reshape(matrix.shape)


def clipped(matrix):
    shaped = matrix.reshape(matrix.shape[0] // QBLK, QBLK, KV_HEADS, HEAD)
    mean_square = jnp.mean(shaped * shaped, axis=(1, 3), keepdims=True)
    clip_bound = clip_ratio * jnp.sqrt(mean_square + 1e-06)
    return jnp.clip(shaped, -clip_bound, clip_bound).reshape(matrix.shape)


def normed_keys(projected, gain):
    shaped = projected.reshape(projected.shape[0], KV_HEADS, HEAD)
    mean_square = jnp.mean(shaped * shaped, axis=-1, keepdims=True)
    return (shaped * lax.rsqrt(mean_square + 1e-06) * gain).reshape(projected.shape)


def scaled(values, block_scales):
    block_count = block_scales.shape[0]
    blocks = values.astype(jnp.float32).reshape(
        block_count, values.shape[0] // block_count, KV_HEADS, HEAD
    )
    return (blocks * block_scales[:, None, :, None]).reshape(values.shape).astype(jnp.bfloat16)


def collect(pieces):
    outer_count = lax.axis_size("gx")
    inner_count = lax.axis_size("gy")
    near_rows = lax.all_gather(pieces, "gx", axis=0, tiled=True)
    gathered = lax.all_gather(near_rows, "gy", axis=0, tiled=True)
    shaped = gathered.reshape(
        (inner_count, outer_count, gathered.shape[0] // (inner_count * outer_count))
        + gathered.shape[1:]
    )
    return jnp.swapaxes(shaped, 0, 1).reshape(gathered.shape)


def body(tokens, codes, scales, gain, cotangent):
    weight = collect(scaled(codes, scales))
    projected = jnp.dot(tokens, weight, preferred_element_type=jnp.float32)
    normed, pullback = jax.vjp(lambda value_in: normed_keys(value_in, gain), projected)
    keys_out = normed.astype(jnp.bfloat16)
    key_grad = pullback(cotangent.astype(jnp.float32))[0].astype(jnp.bfloat16)
    token_grad = lax.dot_general(
        key_grad, weight, (((1,), (1,)), ((), ())), preferred_element_type=jnp.float32
    ).astype(jnp.bfloat16)
    rotation = hadamard(HEAD)
    partial_value = lax.dot_general(
        tokens, key_grad, (((0,), (0,)), ((), ())), preferred_element_type=jnp.float32
    )
    level_one = lax.psum_scatter(
        clipped(rotate(partial_value, rotation)).astype(jnp.bfloat16),
        "gx",
        scatter_dimension=0,
        tiled=True,
    ).astype(jnp.float32)
    recoded = clipped(level_one)
    level_two = lax.psum_scatter(
        recoded.astype(jnp.bfloat16), "gy", scatter_dimension=0, tiled=True
    ).astype(jnp.float32)
    weight_grad = rotate(level_two, rotation)
    return (keys_out, token_grad, weight_grad)


def solution(mesh):
    in_specs = (
        P(("gx", "gy"), None),
        P(("gx", "gy"), None),
        P(("gx", "gy"), None),
        P(),
        P(("gx", "gy"), None),
    )
    out_specs = (P(("gx", "gy"), None), P(("gx", "gy"), None), P(("gx", "gy"), None))
    return jax.shard_map(body, mesh=mesh, in_specs=in_specs, out_specs=out_specs, check_vma=False)
```

profile of v0, /device:TPU:0, one launch (start us, length us, event | category | flops | bytes accessed | tf_op | source)
XLA Modules:
  0.0 265.3 jit_solution(8661850951664697459)
XLA Ops:
  8.0 0.9 fusion.7
  8.9 18.0 %all_gather.6 = bf16[512,512]{1,0:T(8,128)(2,1)} all-gather(bf16[128,512]{1,0:T(8,128)(2,1)S(1)} %fusion.7), channel_id=1, replica_groups=mesh['gx'=4,'gy'=8] {'gx'}, dimensions={0}, use_global_device_ids=true | all-gather | bytes 655360 | tf_op jit(solution)/shard_map/all_gather | solution.py:52
  27.0 1.5 copy.21
  29.2 36.4 %all-gather.2.cloned.1.call-done = bf16[4096,512]{1,0:T(8,128)(2,1)} async-done(((bf16[512,512]{1,0:T(8,128)(2,1)}), bf16[4096,512]{1,0:T(8,128)(2,1)}) %all-gather.2.cloned.1.call-update) | async-done | bytes 4194320 | tf_op jit(solution)/shard_map/all_gather | solution.py:53
  65.6 2.7 %copy.20 = bf16[4,8,128,512]{3,2,1,0:T(8,128)(2,1)S(1)} copy(bf16[4,8,128,512]{3,2,0,1:T(8,128)(2,1)} %bitcast.72) | data formatting | bytes 8388608 | tf_op jit(solution)/shard_map/transpose | solution.py:58
  68.3 3.2 %copy-done.1 = bf16[896,4096]{1,0:T(8,128)(2,1)S(1)} copy-done((bf16[896,4096]{1,0:T(8,128)(2,1)S(1)}, bf16[896,4096]{1,0:T(8,128)(2,1)}, u32[]{:S(2)}) %copy-start.1) | copy-done | bytes 7340056
  71.4 4.7 %multiply_reduce_fusion.1 = (f32[896,4]{0,1:T(4,128)S(1)}, f32[896,4]{0,1:T(4,128)S(1)}, f32[512,896]{1,0:T(8,128)S(1)}) fusion(f32[128]{0:T(128)S(1)} %copy-done.6, bf16[896,512]{0,1:T(8,128)(2,1)S(1)} %copy.21, bf16[4096,512]{1,0:T(8,128)(2,1)S(1)} %bitcast.70, bf16[896,4096]{1,0:T(8,128)(2,1)S(1)} %copy-done.1), kind=kOutput, calls=%fused_computation.18 | convolution fusion | flops 3760841728 | bytes 14316032 | tf_op jit(solution)/shard_map/dot_general | solution.py:63
  76.2 1.5 fusion.4
  77.7 0.9 copy-done.4
  78.7 6.7 %convolution_bitcast_fusion = f32[4096,512]{0,1:T(8,128)} fusion(bf16[896,512]{0,1:T(8,128)(2,1)S(1)} %get-tuple-element.14, bf16[896,4096]{1,0:T(8,128)(2,1)S(1)} %copy-done.1), kind=kOutput, calls=%fused_computation.5 | convolution fusion | flops 3758096384 | bytes 16646144 | tf_op jit(solution)/shard_map/dot_general | solution.py:71
  85.3 9.0 %copy.22 = f32[4096,512]{1,0:T(8,128)} copy(f32[4096,512]{0,1:T(8,128)} %convolution_bitcast_fusion) | data formatting | bytes 16777216 | tf_op jit(solution)/shard_map/dot_general | solution.py:71
  94.3 9.9 %dot_general.26 = f32[128,32,4,128]{3,2,1,0:T(4,128)} reshape(f32[4096,512]{1,0:T(8,128)} %copy.22) | data formatting | bytes 16777216 | tf_op jit(solution)/shard_map/rhc,cd->rhd/dot_general | solution.py:24
  104.2 16.1 %multiply_reduce_fusion = (f32[128,4]{0,1:T(4,128)S(1)}, bf16[128,32,4,128]{0,3,2,1:T(8,128)(2,1)S(1)}) fusion(f32[128,32,4,128]{3,2,1,0:T(4,128)} %dot_general.26), kind=kOutput, calls=%fused_computation.3 | convolution fusion | flops 3228106240 | bytes 12584960 | tf_op jit(solution)/shard_map/rhc,cd->rhd/dot_general | solution.py:24
  120.4 2.3 minimum_convert_fusion
  122.7 7.9 %copy.24 = bf16[128,32,4,128]{3,2,1,0:T(4,128)(2,1)} copy(bf16[128,32,4,128]{0,3,2,1:T(8,128)(2,1)} %minimum_convert_fusion) | data formatting | bytes 8388608 | tf_op jit(solution)/shard_map/convert_element_type | solution.py:75
  130.7 4.9 %copy.43 = bf16[512,8,4,128]{3,1,2,0:T(8,128)(2,1)} copy(bf16[512,8,4,128]{3,2,1,0:T(4,128)(2,1)} %bitcast.69) | data formatting | bytes 8388608
  135.7 76.9 %reduce-scatter.3.cloned.1.call-done = bf16[1024,512]{1,0:T(8,128)(2,1)} async-done(((bf16[4096,512]{1,0:T(8,128)(2,1)}), bf16[1024,512]{1,0:T(8,128)(2,1)}) %reduce-scatter.3.cloned.1.call-update) | async-done | bytes 1048592 | tf_op jit(solution)/shard_map/reduce_scatter | solution.py:74
  212.6 2.8 %convert_multiply_fusion = f32[1024,512]{1,0:T(8,128)} fusion(bf16[1024,512]{1,0:T(8,128)(2,1)} %reduce-scatter.3.cloned.1.call-done), kind=kLoop, calls=%fused_computation.11 | loop fusion | flops 1048576 | bytes 3145728 | tf_op jit(solution)/shard_map/mul | solution.py:30
  215.4 2.0 mul.146
  218.5 1.4 fusion.3
  220.0 1.3 copy.27
  221.3 9.3 %convolution_convert_fusion = bf16[896,4096]{1,0:T(8,128)(2,1)} fusion(bf16[896,512]{0,1:T(8,128)(2,1)S(1)} %copy-done.5, bf16[4096,512]{1,0:T(8,128)(2,1)} %bitcast.71), kind=kOutput, calls=%fused_computation.4 | convolution fusion | flops 3761766400 | bytes 12451840 | tf_op jit(solution)/shard_map/dot_general | solution.py:67
  230.6 26.0 %reduce-scatter.5.cloned.1.call-done = bf16[128,512]{1,0:T(8,128)(2,1)} async-done(((bf16[1024,512]{1,0:T(8,128)(2,1)}), bf16[128,512]{1,0:T(8,128)(2,1)}) %reduce-scatter.5.cloned.1.call-update) | async-done | bytes 131088 | tf_op jit(solution)/shard_map/reduce_scatter | solution.py:81
  256.6 1.0 copy.25
  (28 shorter events, 3.9 us)
Async XLA Ops:
  7.2 58.4 %all-gather.2.cloned.1.call-start = ((), (), s32[]{:S(2)}) async-start(), calls=%async_computation.2 | async-start | bytes 4718592 | tf_op jit(solution)/shard_map/all_gather | solution.py:53
  27.0 185.6 %reduce-scatter.3.cloned.1.call-start = ((), (), s32[]{:S(2)}) async-start(), calls=%async_computation.3 | async-start | bytes 5242880 | tf_op jit(solution)/shard_map/reduce_scatter | solution.py:74
  65.6 5.9 %copy-start.1 = (bf16[896,4096]{1,0:T(8,128)(2,1)S(1)}, bf16[896,4096]{1,0:T(8,128)(2,1)}, u32[]{:S(2)}) copy-start(bf16[896,4096]{1,0:T(8,128)(2,1)} %param.5) | copy-start | bytes 22020100
  65.6 5.9 %copy-start.6 = (f32[128]{0:T(128)S(1)}, f32[128]{0:T(128)}, u32[]{:S(2)}) copy-start(f32[128]{0:T(128)} %param.8) | copy-start | bytes 1540
  68.3 7.9 %copy-start = (bf16[4,8,128,512]{3,2,1,0:T(8,128)(2,1)}, bf16[4,8,128,512]{3,2,1,0:T(8,128)(2,1)S(1)}, u32[]{:S(2)}) copy-start(bf16[4,8,128,512]{3,2,1,0:T(8,128)(2,1)S(1)} %copy.20) | copy-start | bytes 12582916
  77.7 0.9 copy-start.4
  135.6 121.0 %reduce-scatter.5.cloned.1.call-start = ((), (), s32[]{:S(2)}) async-start(), calls=%async_computation.4 | async-start | bytes 1179648 | tf_op jit(solution)/shard_map/reduce_scatter | solution.py:81
  215.4 3.1 %copy-start.2 = (bf16[1024,512]{1,0:T(8,128)(2,1)S(1)}, bf16[1024,512]{1,0:T(8,128)(2,1)}, u32[]{:S(2)}) copy-start(bf16[1024,512]{1,0:T(8,128)(2,1)} %reduce-scatter.3.cloned.1.call-done) | copy-start | bytes 3145732
  217.8 2.2 copy-start.3
  218.2 3.1 %copy-start.5 = (bf16[896,512]{0,1:T(8,128)(2,1)S(1)}, bf16[896,512]{0,1:T(8,128)(2,1)}, u32[]{:S(2)}) copy-start(bf16[896,512]{0,1:T(8,128)(2,1)} %copy-done.4) | copy-start | bytes 2752516
Sparse Core Ops, SparseCore 0:
  27.1 38.4 all-gather.1
  135.7 76.7 reduce-scatter.2
  220.1 36.4 reduce-scatter.4
where the time goes:
time: 266 us; the launch traced here: 265 us
  waiting for transfers between devices  139 us (52%)
  local copies, waits for them, and re-layouts  47.4 us (18%)
  matrix products  37.1 us (14%)
  blocking collectives  18 us (7%)
  between operations  13.9 us (5%)
  other arithmetic  9.49 us (4%)
    reduce_scatter x1, waiting for transfers between devices, body(): lax.psum_scatter(clipped(rotate(partial_value, rotation)).astype(jnp.bflo...  76.9 us
    all_gather x1, waiting for transfers between devices, collect(): gathered = lax.all_gather(near_rows, 'gy', axis=0, tiled=True)  36.4 us
    reduce_scatter x1, waiting for transfers between devices, body(): lax.psum_scatter(recoded.astype(jnp.bfloat16), 'gy', scatter_dimension=0,...  26 us
    all_gather x1, blocking collectives, collect(): near_rows = lax.all_gather(pieces, 'gx', axis=0, tiled=True)  18 us
    dot_general x2, matrix products, rotate(): jnp.einsum('rhc,cd->rhd', shaped, rotation, precision=lax.Precision.HIGHEST)  16.4 us
    unnamed x18, local copies, waits for them, and re-layouts  12.7 us
    dot_general x1, local copies, waits for them, and re-layouts, rotate(): jnp.einsum('rhc,cd->rhd', shaped, rotation, precision=lax.Precision.HIGHEST)  9.9 us
    dot_general x1, matrix products, body(): lax.dot_general(key_grad, weight, (((1,), (1,)), ((), ())), preferred_ele...  9.27 us
  transfers between devices with their start and end apart: 3, of which 3 were waited for; matrix products, arithmetic and copies ran while one was open for 5% of the time, Pallas kernels for 0%

commit v1 on v0

--- a/solution.py
+++ b/solution.py
@@ -49,7 +49,23 @@
 def collect(pieces):
     outer_count = lax.axis_size("gx")
     inner_count = lax.axis_size("gy")
-    near_rows = lax.all_gather(pieces, "gx", axis=0, tiled=True)
+    size, index, extent = (lax.axis_size("gx"), lax.axis_index("gx"), pieces.shape[0])
+    upward = [(i, (i + 1) % size) for i in range(size)]
+    left = [(i, (i - 1) % size) for i in range(size)]
+    near_rows = jnp.zeros((*pieces.shape[:0], size * extent, *pieces.shape[0 + 1 :]), pieces.dtype)
+    near_rows = lax.dynamic_update_slice_in_dim(near_rows, pieces, index * extent, axis=0)
+    from_left = from_right = pieces
+    halfway = size // 2
+    for step in range(1, halfway + 1):
+        from_left = lax.ppermute(from_left, "gx", upward)
+        near_rows = lax.dynamic_update_slice_in_dim(
+            near_rows, from_left, (index - step) % size * extent, axis=0
+        )
+        if step < size - halfway:
+            from_right = lax.ppermute(from_right, "gx", left)
+            near_rows = lax.dynamic_update_slice_in_dim(
+                near_rows, from_right, (index + step) % size * extent, axis=0
+            )
     gathered = lax.all_gather(near_rows, "gy", axis=0, tiled=True)
     shaped = gathered.reshape(
         (inner_count, outer_count, gathered.shape[0] // (inner_count * outer_count))

time: 266 us -> 263 us (0.989)
  blocking collectives: 18 us -> 0 us
  waiting for transfers between devices: 139 us -> 148 us
  starting transfers between devices: 0.12 us -> 5.32 us
    all_gather x1 -> x0, blocking collectives: 18 us -> none  [collect(): near_rows = lax.all_gather(pieces, 'gx', axis=0, tiled=True)]
    ppermute x0 -> x3, waiting for transfers between devices: none -> 11 us  [the longest x2 9.65 us: collect(): from_left = lax.ppermute(from_left, 'gx', upward)]
    ppermute x0 -> x3, starting transfers between devices: none -> 5.2 us  [the longest x2 3.11 us: collect(): from_left = lax.ppermute(from_left, 'gx', upward)]
    unnamed x18 -> x20, local copies, waits for them, and re-layouts: 12.7 us -> 13.5 us
  transfers between devices with their start and end apart: 3 -> 6, of which waited for: 3 -> 6; matrix products, arithmetic and copies ran while one was open for 5% -> 5% of each run, Pallas kernels for 0% -> 0%
where the time goes in v1:
time: 263 us; the launch traced here: 262 us
  waiting for transfers between devices  148 us (56%)
  local copies, waits for them, and re-layouts  47.6 us (18%)
  matrix products  37.1 us (14%)
  between operations  13.9 us (5%)
  other arithmetic  9.49 us (4%)
  starting transfers between devices  5.32 us (2%)
    reduce_scatter x1, waiting for transfers between devices, body(): lax.psum_scatter(clipped(rotate(partial_value, rotation)).astype(jnp.bflo...  76.9 us
    all_gather x1, waiting for transfers between devices, collect(): gathered = lax.all_gather(near_rows, 'gy', axis=0, tiled=True)  34.4 us
    reduce_scatter x1, waiting for transfers between devices, body(): lax.psum_scatter(recoded.astype(jnp.bfloat16), 'gy', scatter_dimension=0,...  26 us
    dot_general x2, matrix products, rotate(): jnp.einsum('rhc,cd->rhd', shaped, rotation, precision=lax.Precision.HIGHEST)  16.4 us
    unnamed x20, local copies, waits for them, and re-layouts  13.5 us
    dot_general x1, local copies, waits for them, and re-layouts, rotate(): jnp.einsum('rhc,cd->rhd', shaped, rotation, precision=lax.Precision.HIGHEST)  9.9 us
    ppermute x2, waiting for transfers between devices, collect(): from_left = lax.ppermute(from_left, 'gx', upward)  9.65 us
    dot_general x1, matrix products, body(): lax.dot_general(key_grad, weight, (((1,), (1,)), ((), ())), preferred_ele...  9.27 us
  transfers between devices with their start and end apart: 6, of which 6 were waited for; matrix products, arithmetic and copies ran while one was open for 5% of the time, Pallas kernels for 0%

profile of v1, /device:TPU:0, one launch (start us, length us, event | category | flops | bytes accessed | tf_op | source)
XLA Modules:
  0.0 261.9 jit_solution(16668729912864642756)
XLA Ops:
  9.0 3.1 %collective-permute-start = (bf16[128,512]{1,0:T(8,128)(2,1)S(1)}, bf16[128,512]{1,0:T(8,128)(2,1)S(1)}, u32[]{:S(2)}, u32[]{:S(2)}) collective-permute-start(bf16[128,512]{1,0:T(8,128)(2,1)S(1)} %get-tuple-element.15), channel_id=1, source_target_pairs={{0,8},{8,16},{16,24},{24,0},{1,9},{9,17},{17,25},{25,1},{2,10},{10... | collective-permute-start | bytes 393224 | tf_op jit(solution)/shard_map/ppermute | solution.py:60
  12.1 2.1 collective-permute-start.1
  14.2 4.3 %collective-permute-done = bf16[128,512]{1,0:T(8,128)(2,1)S(1)} collective-permute-done((bf16[128,512]{1,0:T(8,128)(2,1)S(1)}, bf16[128,512]{1,0:T(8,128)(2,1)S(1)}, u32[]{:S(2)}, u32[]{:S(2)}) %collective-permute-start) | collective-permute-done | bytes 131104 | tf_op jit(solution)/shard_map/ppermute | solution.py:60
  18.5 1.4 collective-permute-done.1
  19.9 5.4 %collective-permute-done.2 = bf16[128,512]{1,0:T(8,128)(2,1)S(1)} collective-permute-done((bf16[128,512]{1,0:T(8,128)(2,1)S(1)}, bf16[128,512]{1,0:T(8,128)(2,1)S(1)}, u32[]{:S(2)}, u32[]{:S(2)}) %collective-permute-start.2) | collective-permute-done | bytes 131104 | tf_op jit(solution)/shard_map/ppermute | solution.py:60
  26.1 1.5 copy.21
  27.7 34.4 %all-gather.2.cloned.1.call-done = bf16[4096,512]{1,0:T(8,128)(2,1)} async-done(((bf16[512,512]{1,0:T(8,128)(2,1)}), bf16[4096,512]{1,0:T(8,128)(2,1)}) %all-gather.2.cloned.1.call-update) | async-done | bytes 4194320 | tf_op jit(solution)/shard_map/all_gather | solution.py:69
  62.1 2.7 %copy.20 = bf16[4,8,128,512]{3,2,1,0:T(8,128)(2,1)S(1)} copy(bf16[4,8,128,512]{3,2,0,1:T(8,128)(2,1)} %bitcast.73) | data formatting | bytes 8388608 | tf_op jit(solution)/shard_map/transpose | solution.py:74
  64.8 3.2 %copy-done.1 = bf16[896,4096]{1,0:T(8,128)(2,1)S(1)} copy-done((bf16[896,4096]{1,0:T(8,128)(2,1)S(1)}, bf16[896,4096]{1,0:T(8,128)(2,1)}, u32[]{:S(2)}) %copy-start.1) | copy-done | bytes 7340056
  68.0 4.7 %multiply_reduce_fusion.1 = (f32[896,4]{0,1:T(4,128)S(1)}, f32[896,4]{0,1:T(4,128)S(1)}, f32[512,896]{1,0:T(8,128)S(1)}) fusion(f32[128]{0:T(128)S(1)} %copy-done.7, bf16[896,512]{0,1:T(8,128)(2,1)S(1)} %copy.21, bf16[4096,512]{1,0:T(8,128)(2,1)S(1)} %bitcast.71, bf16[896,4096]{1,0:T(8,128)(2,1)S(1)} %copy-done.1), kind=kOutput, calls=%fused_computation.18 | convolution fusion | flops 3760841728 | bytes 14316032 | tf_op jit(solution)/shard_map/dot_general | solution.py:79
  72.8 1.5 fusion.4
  75.2 6.7 %convolution_bitcast_fusion = f32[4096,512]{0,1:T(8,128)} fusion(bf16[896,512]{0,1:T(8,128)(2,1)S(1)} %get-tuple-element.16, bf16[896,4096]{1,0:T(8,128)(2,1)S(1)} %copy-done.1), kind=kOutput, calls=%fused_computation.5 | convolution fusion | flops 3758096384 | bytes 16646144 | tf_op jit(solution)/shard_map/dot_general | solution.py:87
  81.9 9.0 %copy.22 = f32[4096,512]{1,0:T(8,128)} copy(f32[4096,512]{0,1:T(8,128)} %convolution_bitcast_fusion) | data formatting | bytes 16777216 | tf_op jit(solution)/shard_map/dot_general | solution.py:87
  90.9 9.9 %dot_general.26 = f32[128,32,4,128]{3,2,1,0:T(4,128)} reshape(f32[4096,512]{1,0:T(8,128)} %copy.22) | data formatting | bytes 16777216 | tf_op jit(solution)/shard_map/rhc,cd->rhd/dot_general | solution.py:24
  100.8 16.1 %multiply_reduce_fusion = (f32[128,4]{0,1:T(4,128)S(1)}, bf16[128,32,4,128]{0,3,2,1:T(8,128)(2,1)S(1)}) fusion(f32[128,32,4,128]{3,2,1,0:T(4,128)} %dot_general.26), kind=kOutput, calls=%fused_computation.3 | convolution fusion | flops 3228106240 | bytes 12584960 | tf_op jit(solution)/shard_map/rhc,cd->rhd/dot_general | solution.py:24
  117.0 2.3 minimum_convert_fusion
  119.3 8.0 %copy.24 = bf16[128,32,4,128]{3,2,1,0:T(4,128)(2,1)} copy(bf16[128,32,4,128]{0,3,2,1:T(8,128)(2,1)} %minimum_convert_fusion) | data formatting | bytes 8388608 | tf_op jit(solution)/shard_map/convert_element_type | solution.py:91
  127.3 4.9 %copy.44 = bf16[512,8,4,128]{3,1,2,0:T(8,128)(2,1)} copy(bf16[512,8,4,128]{3,2,1,0:T(4,128)(2,1)} %bitcast.70) | data formatting | bytes 8388608
  132.3 76.9 %reduce-scatter.3.cloned.1.call-done = bf16[1024,512]{1,0:T(8,128)(2,1)} async-done(((bf16[4096,512]{1,0:T(8,128)(2,1)}), bf16[1024,512]{1,0:T(8,128)(2,1)}) %reduce-scatter.3.cloned.1.call-update) | async-done | bytes 1048592 | tf_op jit(solution)/shard_map/reduce_scatter | solution.py:90
  209.2 2.8 %convert_multiply_fusion = f32[1024,512]{1,0:T(8,128)} fusion(bf16[1024,512]{1,0:T(8,128)(2,1)} %reduce-scatter.3.cloned.1.call-done), kind=kLoop, calls=%fused_computation.11 | loop fusion | flops 1048576 | bytes 3145728 | tf_op jit(solution)/shard_map/mul | solution.py:30
  212.0 2.0 mul.162
  215.1 1.4 fusion.3
  217.9 9.3 %convolution_convert_fusion = bf16[896,4096]{1,0:T(8,128)(2,1)} fusion(bf16[896,512]{0,1:T(8,128)(2,1)S(1)} %copy-done.6, bf16[4096,512]{1,0:T(8,128)(2,1)} %bitcast.72), kind=kOutput, calls=%fused_computation.4 | convolution fusion | flops 3761766400 | bytes 12451840 | tf_op jit(solution)/shard_map/dot_general | solution.py:83
  227.2 26.0 %reduce-scatter.5.cloned.1.call-done = bf16[128,512]{1,0:T(8,128)(2,1)} async-done(((bf16[1024,512]{1,0:T(8,128)(2,1)}), bf16[128,512]{1,0:T(8,128)(2,1)}) %reduce-scatter.5.cloned.1.call-update) | async-done | bytes 131088 | tf_op jit(solution)/shard_map/reduce_scatter | solution.py:97
  (39 shorter events, 8.2 us)
Async XLA Ops:
  7.2 20.5 %copy-start.7 = (f32[128]{0:T(128)S(1)}, f32[128]{0:T(128)}, u32[]{:S(2)}) copy-start(f32[128]{0:T(128)} %param.8) | copy-start | bytes 1540
  7.2 55.0 %all-gather.2.cloned.1.call-start = ((), (), s32[]{:S(2)}) async-start(), calls=%async_computation.2 | async-start | bytes 4718592 | tf_op jit(solution)/shard_map/all_gather | solution.py:69
  9.0 9.5 %collective-permute-start = (bf16[128,512]{1,0:T(8,128)(2,1)S(1)}, bf16[128,512]{1,0:T(8,128)(2,1)S(1)}, u32[]{:S(2)}, u32[]{:S(2)}) collective-permute-start(bf16[128,512]{1,0:T(8,128)(2,1)S(1)} %get-tuple-element.15), channel_id=1, source_target_pairs={{0,8},{8,16},{16,24},{24,0},{1,9},{9,17},{17,25},{25,1},{2,10},{10... | collective-permute-start | bytes 393224 | tf_op jit(solution)/shard_map/ppermute | solution.py:60
  12.1 7.8 %collective-permute-start.1 = (bf16[128,512]{1,0:T(8,128)(2,1)S(1)}, bf16[128,512]{1,0:T(8,128)(2,1)S(1)}, u32[]{:S(2)}, u32[]{:S(2)}) collective-permute-start(bf16[128,512]{1,0:T(8,128)(2,1)S(1)} %get-tuple-element.15), channel_id=1, source_target_pairs={{0,24},{8,0},{16,8},{24,16},{1,25},{9,1},{17,9},{25,17},{2,26},{10... | collective-permute-start | bytes 393224 | tf_op jit(solution)/shard_map/ppermute | solution.py:65
  18.5 6.8 %collective-permute-start.2 = (bf16[128,512]{1,0:T(8,128)(2,1)S(1)}, bf16[128,512]{1,0:T(8,128)(2,1)S(1)}, u32[]{:S(2)}, u32[]{:S(2)}) collective-permute-start(bf16[128,512]{1,0:T(8,128)(2,1)S(1)} %collective-permute-done), channel_id=1, source_target_pairs={{0,8},{8,16},{16,24},{24,0},{1,9},{9,17},{17,25},{25,1},{2,10},{10... | collective-permute-start | bytes 393224 | tf_op jit(solution)/shard_map/ppermute | solution.py:60
  25.3 0.8 copy-start.4
  26.1 183.1 %reduce-scatter.3.cloned.1.call-start = ((), (), s32[]{:S(2)}) async-start(), calls=%async_computation.3 | async-start | bytes 5242880 | tf_op jit(solution)/shard_map/reduce_scatter | solution.py:90
  62.1 5.9 %copy-start.1 = (bf16[896,4096]{1,0:T(8,128)(2,1)S(1)}, bf16[896,4096]{1,0:T(8,128)(2,1)}, u32[]{:S(2)}) copy-start(bf16[896,4096]{1,0:T(8,128)(2,1)} %param.5) | copy-start | bytes 22020100
  64.8 7.9 %copy-start = (bf16[4,8,128,512]{3,2,1,0:T(8,128)(2,1)}, bf16[4,8,128,512]{3,2,1,0:T(8,128)(2,1)S(1)}, u32[]{:S(2)}) copy-start(bf16[4,8,128,512]{3,2,1,0:T(8,128)(2,1)S(1)} %copy.20) | copy-start | bytes 12582916
  74.3 0.9 copy-start.5
  132.2 121.0 %reduce-scatter.5.cloned.1.call-start = ((), (), s32[]{:S(2)}) async-start(), calls=%async_computation.4 | async-start | bytes 1179648 | tf_op jit(solution)/shard_map/reduce_scatter | solution.py:97
  212.0 3.1 %copy-start.2 = (bf16[1024,512]{1,0:T(8,128)(2,1)S(1)}, bf16[1024,512]{1,0:T(8,128)(2,1)}, u32[]{:S(2)}) copy-start(bf16[1024,512]{1,0:T(8,128)(2,1)} %reduce-scatter.3.cloned.1.call-done) | copy-start | bytes 3145732
  214.4 2.2 copy-start.3
  214.8 3.1 %copy-start.6 = (bf16[896,512]{0,1:T(8,128)(2,1)S(1)}, bf16[896,512]{0,1:T(8,128)(2,1)}, u32[]{:S(2)}) copy-start(bf16[896,512]{0,1:T(8,128)(2,1)} %copy-done.5) | copy-start | bytes 2752516
Sparse Core Ops, SparseCore 0:
  26.2 35.8 all-gather.1
  132.4 76.7 reduce-scatter.2
  216.7 36.4 reduce-scatter.4
